TPU v7x, 32 devices: a whole 2x2x4 slice. The times are simulated.
32 devices in a mesh: row: 8 (over z, core), col: 4 (over y, x).
Axes of the slice: x: 2, y: 2, z: 4, core: 2. Of those that a mesh axis runs over, the one named last changes fastest.
Arguments:
- tile_left: bfloat16 [8, 4, 2048, 128], P('row', 'col'), may hold values from -6 to 6
- tile_right: bfloat16 [8, 4, 2048, 128], P('row', 'col'), may hold values from -1 to 1
- tile_blocks: int32 [8, 4], P('row', 'col'), may hold values from 1 to 4
- panel_left: bfloat16 [2, 8, 2048, 128], P(None, 'row', 'col'), may hold values from -6 to 6
- panel_right: bfloat16 [2, 8, 2048, 128], P(None, 'row', 'col'), may hold values from -2 to 2
- swap_flag: int32 [8, 4], P('row', 'col'), may hold values from 0 to 1, as said below
Outputs:
- grown_left: bfloat16 [8, 4, 2048, 256], P('row', 'col')
- grown_right: bfloat16 [8, 4, 2048, 256], P('row', 'col')
Inputs may be any that keep to these rules, and one draw needn't show every extreme that they name: swap_flag[i, c] equals swap_flag[i, (c + 4 / 2) mod 4], so tiles change owner in pairs.
All inputs are finite; a program needn't handle non-finite values.
Results may differ from a plain program's by a relative error of at most 0.0057.
Values may be sent and summed in bfloat16 or wider, within the bound.
A program may use at most 64 MiB of HBM per device.

v0:
```python
import jax
import jax.numpy as jnp
from jax import lax
from jax.sharding import PartitionSpec as P

RBLK = 32


def swapped(value, axis, apart):
    mask = 2**apart
    pairs = [(source, source ^ mask) for source in range(lax.axis_size(axis))]
    return lax.ppermute(value, axis, pairs)


def expand(row_left, masked_left, masked_right, col_left, coupling, live_cols):
    lifted = (-jnp.dot(row_left, coupling, preferred_element_type=jnp.float32)).astype(jnp.bfloat16)
    stacked_left = jnp.concatenate([masked_left, lifted], axis=1)
    stacked_right = jnp.concatenate([masked_right, col_left], axis=1)
    dead_cols = jnp.concatenate(
        [1.0 - live_cols.astype(jnp.float32), jnp.zeros((coupling.shape[1],), jnp.float32)]
    )
    gram_matrix = (
        jnp.dot(stacked_left.T, stacked_left, preferred_element_type=jnp.float32)
        / stacked_left.shape[0]
    )
    gram_matrix = gram_matrix + jnp.diag(dead_cols)
    factor = jnp.linalg.cholesky(gram_matrix)
    left_out = lax.linalg.triangular_solve(
        factor, stacked_left.astype(jnp.float32), left_side=False, lower=True, transpose_a=True
    )
    right_out = jnp.dot(stacked_right.astype(jnp.float32), factor, precision=lax.Precision.HIGHEST)
    return (left_out.astype(jnp.bfloat16), right_out.astype(jnp.bfloat16))


def per_device(tile_left, tile_right, tile_blocks, panel_left, panel_right, swap_flag):
    col_count = lax.axis_size("col")
    own_left, own_right = (
        lax.all_gather(panel_left[1], "col", axis=1, tiled=True),
        lax.all_gather(panel_right[1], "col", axis=1, tiled=True),
    )
    row_left = own_left[0]
    row_right = own_right[0]
    pieces = (
        lax.all_gather(panel_left[0], "row", axis=0, tiled=True),
        lax.all_gather(panel_right[0], "row", axis=0, tiled=True),
    )
    count = pieces[0].shape[0]
    source = lax.iota(jnp.int32, count)
    select = (source[:, None] == lax.iota(jnp.int32, col_count)[None, :]).astype(jnp.bfloat16)
    picked_left = jnp.einsum("kc,kbr->cbr", select, pieces[0], preferred_element_type=jnp.float32)
    picked_right = jnp.einsum("kc,kbr->cbr", select, pieces[1], preferred_element_type=jnp.float32)
    held_left = picked_left.astype(jnp.bfloat16)
    held_right = picked_right.astype(jnp.bfloat16)
    whole_left, whole_right = (
        lax.all_to_all(held_left, "col", split_axis=0, concat_axis=1, tiled=True),
        lax.all_to_all(held_right, "col", split_axis=0, concat_axis=1, tiled=True),
    )
    col_left = whole_left[0]
    col_right = whole_right[0]
    rank_width = tile_left.shape[3]
    live_mask = lax.iota(jnp.int32, rank_width) < tile_blocks[0, 0] * RBLK
    zero_value = jnp.zeros((), jnp.bfloat16)
    masked_left = jnp.where(live_mask[None, :], tile_left[0, 0], zero_value)
    masked_right = jnp.where(live_mask[None, :], tile_right[0, 0], zero_value)
    coupling = jnp.dot(row_right.T, col_right, preferred_element_type=jnp.float32).astype(
        jnp.bfloat16
    )
    live_cols = live_mask.astype(jnp.bfloat16)
    partner_bit = col_count.bit_length() - 2
    flagged = swap_flag[0, 0] == 1
    left_out, right_out = expand(row_left, masked_left, masked_right, col_left, coupling, live_cols)
    other_left, other_right = swapped((left_out, right_out), "col", partner_bit)
    left_out = jnp.where(flagged, other_left, left_out)
    right_out = jnp.where(flagged, other_right, right_out)
    return (left_out[None, None], right_out[None, None])


def solution(mesh):
    placed = (
        P("row", "col", None, None),
        P("row", "col", None, None),
        P("row", "col"),
        P(None, "row", "col", None),
        P(None, "row", "col", None),
        P("row", "col"),
    )
    return jax.shard_map(
        per_device,
        mesh=mesh,
        in_specs=placed,
        out_specs=(P("row", "col", None, None), P("row", "col", None, None)),
        check_vma=False,
    )
```

profile of v0, /device:TPU:0, one launch (start us, length us, event | category | flops | bytes accessed | tf_op | source)
XLA Modules:
  0.0 188.6 jit_solution(15129123731806882609)
XLA Ops:
  7.2 1.7 fusion.38
  9.0 1.7 fusion.37
  11.8 11.5 %all-gather.2 = bf16[1,1,2048,128]{3,2,1,0:T(8,128)(2,1)S(1)} all-gather(bf16[1,1,512,128]{3,2,1,0:T(8,128)(2,1)S(1)} %get-tuple-element.27), channel_id=4, replica_groups=mesh['row'=8,'col'=4] {'col'}, dimensions={2}, use_global_device_ids=true | all-gather | bytes 655360 | tf_op jit(solution)/shard_map/all_gather | solution.py:38
  23.3 1.1 bitcast_select_fusion
  24.4 10.7 %all-gather.7.cloned.1.call-done = bf16[8,1,512,128]{3,2,1,0:T(8,128)(2,1)} async-done(((bf16[1,1,512,128]{3,2,1,0:T(8,128)(2,1)}), bf16[8,1,512,128]{3,2,1,0:T(8,128)(2,1)}) %all-gather.7.cloned.1.call-update) | async-done | bytes 1048592 | tf_op jit(solution)/shard_map/all_gather | solution.py:45
  35.1 2.0 %convolution_convert_fusion.3 = bf16[4,512,128]{2,0,1:T(4,128)(2,1)S(1)} fusion(bf16[8,1,512,128]{3,2,1,0:T(8,128)(2,1)} %all-gather.7.cloned.1.call-done), kind=kOutput, calls=%fused_computation.9 | convolution fusion | flops 4456480 | bytes 1572864 | tf_op jit(solution)/shard_map/kc,kbr->cbr/dot_general | solution.py:51
  37.1 0.9 copy.29
  38.0 3.7 %all-to-all-start = ((bf16[4,512,128]{2,1,0:T(8,128)(2,1)}), bf16[4,512,128]{2,1,0:T(8,128)(2,1)S(1)}, u32[]{:S(2)}, u32[]{:S(2)}) async-start(bf16[4,512,128]{2,1,0:T(8,128)(2,1)} %copy.29), calls=%async_computation | async-start | bytes 1048576 | tf_op jit(solution)/shard_map/all_to_all | solution.py:56
  41.6 14.3 %all-gather.1 = bf16[1,1,2048,128]{3,2,1,0:T(8,128)(2,1)S(1)} all-gather(bf16[1,1,512,128]{3,2,1,0:T(8,128)(2,1)S(1)} %get-tuple-element.28), channel_id=3, replica_groups=mesh['row'=8,'col'=4] {'col'}, dimensions={2}, use_global_device_ids=true | all-gather | bytes 655360 | tf_op jit(solution)/shard_map/all_gather | solution.py:39
  55.9 2.7 %all-gather.9.cloned.1.call-done = bf16[8,1,512,128]{3,2,1,0:T(8,128)(2,1)} async-done(((bf16[1,1,512,128]{3,2,1,0:T(8,128)(2,1)}), bf16[8,1,512,128]{3,2,1,0:T(8,128)(2,1)}) %all-gather.9.cloned.1.call-update) | async-done | bytes 1048592 | tf_op jit(solution)/shard_map/all_gather | solution.py:44
  58.6 2.0 %convolution_convert_fusion.2 = bf16[4,512,128]{2,0,1:T(4,128)(2,1)S(1)} fusion(bf16[8,1,512,128]{3,2,1,0:T(8,128)(2,1)} %all-gather.9.cloned.1.call-done), kind=kOutput, calls=%fused_computation.8 | convolution fusion | flops 4456480 | bytes 1572864 | tf_op jit(solution)/shard_map/kc,kbr->cbr/dot_general | solution.py:50
  60.6 0.9 copy.34
  61.5 3.7 %all-to-all-start.1 = ((bf16[4,512,128]{2,1,0:T(8,128)(2,1)}), bf16[4,512,128]{2,1,0:T(8,128)(2,1)S(1)}, u32[]{:S(2)}, u32[]{:S(2)}) async-start(bf16[4,512,128]{2,1,0:T(8,128)(2,1)} %copy.34), calls=%async_computation.1 | async-start | bytes 1048576 | tf_op jit(solution)/shard_map/all_to_all | solution.py:55
  65.7 1.7 convolution_multiply_fusion
  67.7 11.7 %cholesky.49 = f32[128,128]{1,0:T(8,128)S(1)} custom-call(f32[128,128]{1,0:T(8,128)S(1)} %cholesky.115), custom_call_target="Cholesky" | custom-call | tf_op jit(solution)/shard_map/jit(cholesky)/cholesky | solution.py:27
  79.4 9.8 %custom-call.14 = f32[1,128,128]{1,2,0:T(8,128)S(1)} custom-call(f32[1,128,128]{2,1,0:T(8,128)S(1)} %get-tuple-element.33), custom_call_target="InvertDiagBlocksLowerTriangular" | custom-call | tf_op jit(solution)/shard_map/jit(cholesky)/cholesky | solution.py:27
  89.7 11.7 %cholesky.103 = f32[128,128]{1,0:T(8,128)S(1)} custom-call(f32[128,128]{1,0:T(8,128)S(1)} %convolution_subtract_fusion.1), custom_call_target="Cholesky" | custom-call | tf_op jit(solution)/shard_map/jit(cholesky)/cholesky | solution.py:27
  103.5 3.8 %while.1 = (s32[]{:T(128)}, f32[256,256]{1,0:T(8,128)S(1)}, s32[2,2]{1,0:T(2,128)S(1)}, f32[2,128,128]{2,1,0:T(8,128)S(1)}, s32[]{:T(128)}) while((s32[]{:T(128)}, f32[256,256]{1,0:T(8,128)S(1)}, s32[2,2]{1,0:T(2,128)S(1)}, f32[2,128,128]{2,1,0:T(8,128)S(1)}, s32[]{:T(128)}) %tuple.34), condition=%wide.while_cond, body=%wide.while_body.sunk | while | flops 2 | bytes 131189 | solution.py:28
  104.1 1.3 bitcast_dynamic-update-slice_fusion.2
  106.0 1.3 bitcast_dynamic-update-slice_fusion.2
  107.3 19.9 %custom-call.15 = f32[2,128,128]{1,2,0:T(8,128)S(1)} custom-call(f32[2,128,128]{2,1,0:T(8,128)S(1)} %get-tuple-element.9), custom_call_target="InvertDiagBlocksLowerTriangular" | custom-call | tf_op jit(solution)/shard_map/triangular_solve | solution.py:28
  127.8 1.1 convolution_subtract_fusion
  128.9 1.1 convolution_convert_fusion.1
  130.0 1.1 pad_maximum_fusion
  131.1 2.0 %collective-permute-start = (bf16[2048,256]{0,1:T(8,128)(2,1)}, bf16[2048,256]{0,1:T(8,128)(2,1)}, u32[]{:S(2)}, u32[]{:S(2)}) collective-permute-start(bf16[2048,256]{0,1:T(8,128)(2,1)} %pad_maximum_fusion), channel_id=1, source_target_pairs={{0,2},{1,3},{2,0},{3,1},{4,6},{5,7},{6,4},{7,5},{8,10},{9,11},{10,... | collective-permute-start | bytes 3145736 | tf_op jit(solution)/shard_map/ppermute | solution.py:12
  133.3 2.0 %convolution_convert_fusion = bf16[2048,256]{0,1:T(8,128)(2,1)} fusion(bf16[2048,128]{0,1:T(8,128)(2,1)S(1)} %copy.41, bf16[2048,128]{0,1:T(8,128)(2,1)S(1)} %copy-done.1, f32[256,256]{1,0:T(8,128)S(1)} %get-tuple-element.31, pred[]{:T(512)S(6)} %cholesky.108), kind=kOutput, calls=%fused_computation.2 | convolution fusion | flops 1613430784 | bytes 2359297 | tf_op jit(solution)/shard_map/dot_general | solution.py:31
  136.8 20.6 %collective-permute-done = bf16[2048,256]{0,1:T(8,128)(2,1)} collective-permute-done((bf16[2048,256]{0,1:T(8,128)(2,1)}, bf16[2048,256]{0,1:T(8,128)(2,1)}, u32[]{:S(2)}, u32[]{:S(2)}) %collective-permute-start) | collective-permute-done | bytes 1048608 | tf_op jit(solution)/shard_map/ppermute | solution.py:12
  157.4 1.6 select_bitcast_fusion.1
  159.0 1.3 copy.37
  160.3 18.8 %collective-permute-done.1 = bf16[2048,256]{0,1:T(8,128)(2,1)} collective-permute-done((bf16[2048,256]{0,1:T(8,128)(2,1)}, bf16[2048,256]{0,1:T(8,128)(2,1)}, u32[]{:S(2)}, u32[]{:S(2)}) %collective-permute-start.1) | collective-permute-done | bytes 1048608 | tf_op jit(solution)/shard_map/ppermute | solution.py:12
  179.1 1.3 select_bitcast_fusion
  180.5 1.3 copy.38
  (38 shorter events, 5.5 us)
Async XLA Ops:
  7.2 3.5 %copy-start.2 = (bf16[1,1,2048,128]{3,2,1,0:T(8,128)(2,1)S(1)}, bf16[1,1,2048,128]{3,2,1,0:T(8,128)(2,1)}, u32[]{:S(2)}) copy-start(bf16[1,1,2048,128]{3,2,1,0:T(8,128)(2,1)} %param.7) | copy-start | bytes 1572868
  7.2 28.0 %all-gather.7.cloned.1.call-start = ((), (), s32[]{:S(2)}) async-start(), calls=%async_computation.2 | async-start | bytes 1179648 | tf_op jit(solution)/shard_map/all_gather | solution.py:45
  8.9 2.7 %copy-start = (bf16[1,1,2048,128]{3,2,1,0:T(8,128)(2,1)S(1)}, bf16[1,1,2048,128]{3,2,1,0:T(8,128)(2,1)}, u32[]{:S(2)}) copy-start(bf16[1,1,2048,128]{3,2,1,0:T(8,128)(2,1)} %param.6) | copy-start | bytes 1572868
  8.9 49.7 %all-gather.9.cloned.1.call-start = ((), (), s32[]{:S(2)}) async-start(), calls=%async_computation.3 | async-start | bytes 1179648 | tf_op jit(solution)/shard_map/all_gather | solution.py:44
  38.0 23.5 %all-to-all-start = ((bf16[4,512,128]{2,1,0:T(8,128)(2,1)}), bf16[4,512,128]{2,1,0:T(8,128)(2,1)S(1)}, u32[]{:S(2)}, u32[]{:S(2)}) async-start(bf16[4,512,128]{2,1,0:T(8,128)(2,1)} %copy.29), calls=%async_computation | async-start | bytes 1048576 | tf_op jit(solution)/shard_map/all_to_all | solution.py:56
  61.5 71.6 %all-to-all-start.1 = ((bf16[4,512,128]{2,1,0:T(8,128)(2,1)}), bf16[4,512,128]{2,1,0:T(8,128)(2,1)S(1)}, u32[]{:S(2)}, u32[]{:S(2)}) async-start(bf16[4,512,128]{2,1,0:T(8,128)(2,1)} %copy.34), calls=%async_computation.1 | async-start | bytes 1048576 | tf_op jit(solution)/shard_map/all_to_all | solution.py:55
  131.1 2.3 %copy-start.1 = (bf16[2048,128]{0,1:T(8,128)(2,1)S(1)}, bf16[2048,128]{0,1:T(8,128)(2,1)}, u32[]{:S(2)}) copy-start(bf16[2048,128]{0,1:T(8,128)(2,1)} %get-tuple-element.34) | copy-start | bytes 1572868
  131.1 26.4 %collective-permute-start = (bf16[2048,256]{0,1:T(8,128)(2,1)}, bf16[2048,256]{0,1:T(8,128)(2,1)}, u32[]{:S(2)}, u32[]{:S(2)}) collective-permute-start(bf16[2048,256]{0,1:T(8,128)(2,1)} %pad_maximum_fusion), channel_id=1, source_target_pairs={{0,2},{1,3},{2,0},{3,1},{4,6},{5,7},{6,4},{7,5},{8,10},{9,11},{10,... | collective-permute-start | bytes 3145736 | tf_op jit(solution)/shard_map/ppermute | solution.py:12
  135.4 43.8 %collective-permute-start.1 = (bf16[2048,256]{0,1:T(8,128)(2,1)}, bf16[2048,256]{0,1:T(8,128)(2,1)}, u32[]{:S(2)}, u32[]{:S(2)}) collective-permute-start(bf16[2048,256]{0,1:T(8,128)(2,1)} %convolution_convert_fusion), channel_id=1, source_target_pairs={{0,2},{1,3},{2,0},{3,1},{4,6},{5,7},{6,4},{7,5},{8,10},{9,11},{10,... | collective-permute-start | bytes 3145736 | tf_op jit(solution)/shard_map/ppermute | solution.py:12
Sparse Core Ops, SparseCore 0:
  10.2 24.9 all-gather.6
  36.7 21.8 all-gather.8
where the time goes:
time: 189 us
  other arithmetic  59.1 us (31%)
  waiting for transfers between devices  52.8 us (28%)
  blocking collectives  25.8 us (14%)
  between operations  16.8 us (9%)
  local copies, waits for them, and re-layouts  12.4 us (7%)
  matrix products  11.5 us (6%)
  starting transfers between devices  10.2 us (5%)
    ppermute x2, waiting for transfers between devices, swapped(): return lax.ppermute(value, axis, pairs)  39.4 us
    another operation x6, other arithmetic, expand(): factor = jnp.linalg.cholesky(gram_matrix)  34 us
    another operation x4, other arithmetic, expand(): lax.linalg.triangular_solve(factor, stacked_left.astype(jnp.float32), lef...  21 us
    all_gather x1, blocking collectives, per_device(): lax.all_gather(panel_right[1], 'col', axis=1, tiled=True)  14.3 us
    all_gather x1, blocking collectives, per_device(): lax.all_gather(panel_left[1], 'col', axis=1, tiled=True)  11.5 us
    all_gather x1, waiting for transfers between devices, per_device(): lax.all_gather(panel_right[0], 'row', axis=0, tiled=True)  10.7 us
    another operation x6, local copies, waits for them, and re-layouts  3.78 us
  transfers between devices with their start and end apart: 6, of which 4 were waited for; matrix products, arithmetic and copies ran while one was open for 42% of the time, Pallas kernels for 0%

commit v1 on v0

v1 whole, which is shorter than its diff:
```python
import functools

import jax
import jax.numpy as jnp
from jax import lax
from jax.experimental import pallas as pl
from jax.experimental.pallas import tpu as pltpu
from jax.sharding import PartitionSpec as P

RBLK = 32
MESH = pl.DeviceIdType.MESH
BF16 = jnp.bfloat16
F32 = jnp.float32


def exchange(R, C, u, v, pleft, pright, meta, uo, vo, rowo, colo, coupo, metao,
             ubuf, vbuf, rowbuf, colbuf, prbuf, psend, precv, mbuf,
             s_swap, r_swap, s_row, r_row, s_col, r_col, s_st, s_pr, r_pr, s_part, r_part, s_meta, r_meta, s_loc):
    r, c = lax.axis_index("row"), lax.axis_index("col")
    half = C // 2
    mate = lax.rem(c + half, C)
    sib = r + 1 - 2 * lax.rem(r, 2)
    has_up, has_dn = r + 2 < R, r >= 2

    def rcopy(src, dst, ss, rs, to):
        return pltpu.make_async_remote_copy(
            src_ref=src, dst_ref=dst, send_sem=ss, recv_sem=rs, device_id=to, device_id_type=MESH
        )

    barrier = pltpu.get_barrier_semaphore()
    for d in range(C):
        @pl.when(d != c)
        def _():
            pl.semaphore_signal(barrier, inc=1, device_id=(r, d), device_id_type=MESH)
    pl.semaphore_signal(barrier, inc=1, device_id=(sib, c), device_id_type=MESH)

    @pl.when(has_up)
    def _():
        pl.semaphore_signal(barrier, inc=1, device_id=(r + 2, c), device_id_type=MESH)

    @pl.when(has_dn)
    def _():
        pl.semaphore_signal(barrier, inc=1, device_id=(r - 2, c), device_id_type=MESH)

    peers = C + jnp.where(has_up, 1, 0) + jnp.where(has_dn, 1, 0)
    pl.semaphore_wait(barrier, peers)

    ends = []

    def send(cond, copy):
        @pl.when(cond)
        def _():
            copy.start()
        ends.append((cond, copy))

    loc_pr = pltpu.make_async_copy(pright.at[0], prbuf.at[lax.min(r, C - 1)], s_loc.at[0])
    is_src_pr = r < C

    def relay_sends(s, src, slot, ss, rs):
        par = lax.rem(r, 2) == lax.rem(s, 2)
        send(par & (r >= s) & has_up, rcopy(src, slot, ss.at[0], rs, (r + 2, c)))
        send(par & (r <= s) & has_dn, rcopy(src, slot, ss.at[1], rs, (r - 2, c)))
        send(par, rcopy(src, slot, ss.at[2], rs, (sib, c)))

    for d in range(C):
        send(c != d, rcopy(meta, mbuf.at[c], s_meta.at[d], r_meta.at[c], (r, d)))

    for s in range(C):
        slot, rs, ss = prbuf.at[s], r_pr.at[s], s_pr.at[s]
        send((r == s) & has_up, rcopy(pright.at[0], slot, ss.at[0], rs, (r + 2, c)))
        send((r == s) & has_dn, rcopy(pright.at[0], slot, ss.at[1], rs, (r - 2, c)))
        send(r == s, rcopy(pright.at[0], slot, ss.at[2], rs, (sib, c)))

    @pl.when(is_src_pr)
    def _():
        loc_pr.start()

    for t in range(2):
        d = lax.rem(r + t * half, C)
        send((r < C) & (d != c), rcopy(pleft.at[0], colbuf.at[t, c], s_st.at[t], r_col.at[t, c], (r, d)))
    tiles = (c, mate)
    loc_pl = []
    for t in range(2):
        copy = pltpu.make_async_copy(pleft.at[0], colbuf.at[t, c], s_loc.at[1 + t])
        loc_pl.append(copy)

        @pl.when(r == tiles[t])
        def _():
            copy.start()

    for d in range(C):
        send(c != d, rcopy(pleft.at[1], rowbuf.at[c], s_row.at[d], r_row.at[c], (r, d)))

    swap_u = rcopy(u, ubuf, s_swap.at[0], r_swap.at[0], (r, mate))
    swap_v = rcopy(v, vbuf, s_swap.at[1], r_swap.at[1], (r, mate))
    swap_u.start()
    swap_v.start()

    for s in range(C):
        slot, rs, ss = prbuf.at[s], r_pr.at[s], s_pr.at[s]

        @pl.when(r != s)
        def _():
            rcopy(slot, slot, ss.at[0], rs, (sib, c)).wait_recv()

        par = lax.rem(r, 2) == s % 2
        send(par & (r > s) & has_up, rcopy(slot, slot, ss.at[0], rs, (r + 2, c)))
        send(par & (r < s) & has_dn, rcopy(slot, slot, ss.at[1], rs, (r - 2, c)))
        send(par & (r != s), rcopy(slot, slot, ss.at[2], rs, (sib, c)))

    @pl.when(is_src_pr)
    def _():
        loc_pr.wait()

    for d in range(C):
        @pl.when(c != d)
        def _():
            rcopy(meta, mbuf.at[d], s_meta.at[d], r_meta.at[d], (r, d)).wait_recv()

        @pl.when(c == d)
        def _():
            mbuf[d] = meta[...]

    part = [
        lax.dot_general(pright[1], prbuf[s], (((0,), (0,)), ((), ())), preferred_element_type=F32)
        for s in range(C)
    ]
    for d in range(C):
        chosen = mbuf[d][0:1, :] > 0.5
        value = jnp.where(chosen, part[(d + half) % C], part[d])
        psend[d] = value

        @pl.when(c == d)
        def _():
            precv[d] = value
    for d in range(C):
        send(c != d, rcopy(psend.at[d], precv.at[c], s_part.at[d], r_part.at[c], (r, d)))

    for b in range(C):
        for t in range(2):
            slot, rs, ss = colbuf.at[t, b], r_col.at[t, b], s_col.at[t, b]
            mine = (r == tiles[t]) & (c == b)

            @pl.when(mine)
            def _():
                loc_pl[t].wait()

            @pl.when(jnp.logical_not(mine))
            def _():
                rcopy(slot, slot, ss.at[0], rs, (sib, c)).wait_recv()

            relay_sends(tiles[t], slot, slot, ss, rs)

    own_meta = meta[...]
    flagged = own_meta[0:1, :] > 0.5

    for d in range(C):
        @pl.when(c != d)
        def _():
            rcopy(pleft.at[1], rowbuf.at[d], s_row.at[d], r_row.at[d], (r, d)).wait_recv()
            rowo[d] = rowbuf[d]

        @pl.when(c == d)
        def _():
            rowo[d] = pleft[1]

    for b in range(C):
        colo[b] = jnp.where(flagged, colbuf[1, b], colbuf[0, b])

    swap_u.wait_recv()
    uo[...] = jnp.where(flagged, ubuf[...], u[...])
    swap_v.wait_recv()
    vo[...] = jnp.where(flagged, vbuf[...], v[...])
    for d in range(C):
        @pl.when(c != d)
        def _():
            rcopy(psend.at[d], precv.at[d], s_part.at[d], r_part.at[d], (r, d)).wait_recv()
    total = precv[0]
    for d in range(1, C):
        total = total + precv[d]
    coupo[...] = total.astype(BF16)
    metao[...] = jnp.where(flagged, mbuf[mate], own_meta)

    swap_u.wait_send()
    swap_v.wait_send()
    for cond, copy in ends:
        @pl.when(cond)
        def _():
            copy.wait_send()


def split3(x):
    h = x.astype(BF16)
    rest = x - h.astype(F32)
    m = rest.astype(BF16)
    return h, m, (rest - m.astype(F32)).astype(BF16)


def factor_rows(work, n, sb):
    lanes = 128
    sub = lax.broadcasted_iota(jnp.int32, (8, lanes), 0)
    groups = sb // 8

    def sub_row(x, k):
        return jnp.broadcast_to(x[k : k + 1, :], x.shape)

    for r0 in range(0, n, sb):
        a0 = r0 // lanes * lanes
        width = n + lanes
        tiles = width // lanes
        rows = [
            [work[r0 + 8 * g : r0 + 8 * g + 8, a0 + lanes * w : a0 + lanes * (w + 1)] for w in range(tiles)]
            for g in range(groups)
        ]
        for t in range(groups):
            base = r0 - a0 + 8 * t
            cols = [
                {g: jnp.broadcast_to(rows[g][0][:, base + i : base + i + 1], (8, lanes)) for g in range(t, groups)}
                for i in range(8)
            ]
            for k in range(8):
                inv = lax.rsqrt(sub_row(cols[k][t], k))
                scaled = {g: cols[k][g] * inv for g in range(t, groups)}
                for j in range(k + 1, 8):
                    lj = sub_row(scaled[t], j)
                    for g in range(t, groups):
                        cols[j][g] = cols[j][g] - scaled[g] * lj
                below = jnp.where(sub > k, scaled[t], 0.0)
                for w in range(tiles):
                    rowk = sub_row(rows[t][w], k) * inv
                    rows[t][w] = jnp.where(sub == k, rowk, rows[t][w] - below * rowk)
                    for g in range(t + 1, groups):
                        rows[g][w] = rows[g][w] - scaled[g] * rowk
        done = jnp.concatenate([jnp.concatenate(rows[g], axis=1) for g in range(groups)], axis=0)
        work[r0 : r0 + sb, a0 : a0 + width] = done
        r1 = r0 + sb
        if r1 < n:
            b0 = r1 // lanes * lanes
            h, m, l = split3(done)
            left = jnp.concatenate([h, h, m, m, h, l], axis=0)[:, b0 - a0 : n - a0]
            right = jnp.concatenate([h, m, h, m, l, h], axis=0)
            update = lax.dot_general(left, right, (((0,), (0,)), ((), ())), preferred_element_type=F32)
            work[r1:n, a0 : a0 + width] = work[r1:n, a0 : a0 + width] - update[r1 - b0 :, :]


def compute(chunk, u, v, row, col, coup, meta, lo, ro, stack, work):
    nb, rk = u.shape
    rp = coup.shape[1]
    n = rk + rp
    lane = lax.broadcasted_iota(jnp.int32, (1, rk), 1).astype(F32)
    live = lane < meta[1:2, :] * RBLK

    def fill(step, acc):
        at = pl.ds(pl.multiple_of(step * chunk, chunk), chunk)
        lifted = -jnp.dot(row[at, :], coup[...], preferred_element_type=F32)
        piece = jnp.concatenate(
            [jnp.where(live, u[at, :], jnp.zeros((), BF16)), lifted.astype(BF16)], axis=1
        )
        stack[at, :] = piece
        return acc + lax.dot_general(piece, piece, (((0,), (0,)), ((), ())), preferred_element_type=F32)

    gram = lax.fori_loop(0, nb // chunk, fill, jnp.zeros((n, n), F32)) / nb
    ri = lax.broadcasted_iota(jnp.int32, (n, n), 0)
    ci = lax.broadcasted_iota(jnp.int32, (n, n), 1)
    dead = jnp.concatenate([jnp.where(live, 0.0, 1.0).astype(F32), jnp.zeros((1, rp), F32)], axis=1)
    work[:, :n] = gram + jnp.where(ri == ci, dead, 0.0)
    work[:, n:] = jnp.where(ri == ci, 1.0, 0.0).astype(F32)
    factor_rows(work, n, 32)
    upper = jnp.where(ri <= ci, work[:, :n], 0.0)
    inverse = work[:, n:]
    uh, um, _ = split3(upper)
    ih, im, _ = split3(inverse)
    nt = (((1,), (1,)), ((), ()))

    def emit(step, _):
        at = pl.ds(pl.multiple_of(step * chunk, chunk), chunk)
        x = stack[at, :]
        left = lax.dot_general(x, ih, nt, preferred_element_type=F32)
        left = left + lax.dot_general(x, im, nt, preferred_element_type=F32)
        lo[at, :] = left.astype(BF16)
        y = jnp.concatenate([jnp.where(live, v[at, :], jnp.zeros((), BF16)), col[at, :]], axis=1)
        right = lax.dot_general(y, uh, nt, preferred_element_type=F32)
        right = right + lax.dot_general(y, um, nt, preferred_element_type=F32)
        ro[at, :] = right.astype(BF16)
        return 0

    lax.fori_loop(0, nb // chunk, emit, 0)


def per_device(R, C, tile_left, tile_right, tile_blocks, panel_left, panel_right, swap_flag):
    nb, rk = tile_left.shape[2:]
    blk, rp = panel_left.shape[2:]
    top = lax.broadcasted_iota(jnp.int32, (8, 128), 0) == 0
    meta = jnp.where(top, swap_flag[0, 0], tile_blocks[0, 0]).astype(F32)
    vm = pl.BlockSpec(memory_space=pltpu.VMEM)
    dma = pltpu.SemaphoreType.DMA
    S = jax.ShapeDtypeStruct
    uo, vo, rowo, colo, coup, metao = pl.pallas_call(
        functools.partial(exchange, R, C),
        out_shape=(
            S((nb, rk), BF16), S((nb, rk), BF16), S((C, blk, rp), BF16), S((C, blk, rp), BF16),
            S((rp, rp), BF16), S((8, 128), F32),
        ),
        in_specs=[vm] * 5,
        out_specs=[vm] * 6,
        scratch_shapes=[
            pltpu.VMEM((nb, rk), BF16), pltpu.VMEM((nb, rk), BF16),
            pltpu.VMEM((C, blk, rp), BF16), pltpu.VMEM((2, C, blk, rp), BF16), pltpu.VMEM((C, blk, rp), BF16),
            pltpu.VMEM((C, rp, rp), F32), pltpu.VMEM((C, rp, rp), F32), pltpu.VMEM((C, 8, 128), F32),
            dma((2,)), dma((2,)), dma((C,)), dma((C,)), dma((2, C, 3)), dma((2, C)), dma((2,)),
            dma((C, 3)), dma((C,)), dma((C,)), dma((C,)), dma((C,)), dma((C,)), dma((3,)),
        ],
        compiler_params=pltpu.CompilerParams(
            collective_id=0, has_side_effects=True, vmem_limit_bytes=40 * 1024 * 1024
        ),
        name="exchange",
    )(tile_left[0, 0], tile_right[0, 0], panel_left[:, 0], panel_right[:, 0], meta)
    n = rk + rp
    lo, ro = pl.pallas_call(
        functools.partial(compute, min(512, nb)),
        out_shape=(S((nb, n), BF16), S((nb, n), BF16)),
        in_specs=[vm] * 6,
        out_specs=[vm] * 2,
        scratch_shapes=[pltpu.VMEM((nb, n), BF16), pltpu.VMEM((n, 2 * n), F32)],
        compiler_params=pltpu.CompilerParams(vmem_limit_bytes=40 * 1024 * 1024),
        name="compute",
    )(uo, vo, rowo.reshape(nb, rp), colo.reshape(nb, rp), coup, metao)
    return lo[None, None], ro[None, None]


def solution(mesh):
    placed = (
        P("row", "col", None, None),
        P("row", "col", None, None),
        P("row", "col"),
        P(None, "row", "col", None),
        P(None, "row", "col", None),
        P("row", "col"),
    )
    return jax.shard_map(
        functools.partial(per_device, mesh.shape["row"], mesh.shape["col"]),
        mesh=mesh,
        in_specs=placed,
        out_specs=(P("row", "col", None, None), P("row", "col", None, None)),
        check_vma=False,
    )
```

time: 189 us -> 70.4 us (0.37)
  the two profiles are of different devices: /device:TPU:0 before, /device:TPU:29 now
where the time goes in v1:
time: 70.4 us; the launch traced here: 70.1 us
  Pallas kernels  64.1 us (91%)
  local copies, waits for them, and re-layouts  4.05 us (6%)
  between operations  1.94 us (3%)
    pallas_call x1, Pallas kernels, per_device(): pl.pallas_call(functools.partial(exchange, R, C), out_shape=(S((nb, rk),...  51.6 us
    pallas_call x1, Pallas kernels, per_device(): pl.pallas_call(functools.partial(compute, min(512, nb)), out_shape=(S((nb...  12.5 us
    unnamed x8, local copies, waits for them, and re-layouts  3.98 us

profile of v1, /device:TPU:29, one launch (start us, length us, event | category | flops | bytes accessed | tf_op | source)
XLA Modules:
  0.0 70.1 jit_solution(1844961942610523106)
XLA Ops:
  1.9 0.1 iota.7.meta
  2.0 0.0 copy-start
  2.0 1.0 %copy-done = bf16[1,1,2048,128]{3,2,1,0:T(8,128)(2,1)S(1)} copy-done((bf16[1,1,2048,128]{3,2,1,0:T(8,128)(2,1)S(1)}, bf16[1,1,2048,128]{3,2,1,0:T(8,128)(2,1)}, u32[]{:S(2)}) %copy-start) | copy-done | bytes 524312
  3.0 0.0 copy-start.1
  3.0 1.0 %copy-done.1 = bf16[1,1,2048,128]{3,2,1,0:T(8,128)(2,1)S(1)} copy-done((bf16[1,1,2048,128]{3,2,1,0:T(8,128)(2,1)S(1)}, bf16[1,1,2048,128]{3,2,1,0:T(8,128)(2,1)}, u32[]{:S(2)}) %copy-start.1) | copy-done | bytes 524312
  4.1 0.0 copy-start.2
  4.1 0.9 %copy-done.2 = bf16[2,1,512,128]{3,2,1,0:T(8,128)(2,1)S(1)} copy-done((bf16[2,1,512,128]{3,2,1,0:T(8,128)(2,1)S(1)}, bf16[2,1,512,128]{3,2,1,0:T(8,128)(2,1)}, u32[]{:S(2)}) %copy-start.2) | copy-done | bytes 262168
  5.0 0.0 copy-start.3
  5.0 0.9 %copy-done.3 = bf16[2,1,512,128]{3,2,1,0:T(8,128)(2,1)S(1)} copy-done((bf16[2,1,512,128]{3,2,1,0:T(8,128)(2,1)S(1)}, bf16[2,1,512,128]{3,2,1,0:T(8,128)(2,1)}, u32[]{:S(2)}) %copy-start.3) | copy-done | bytes 262168
  6.0 51.6 %exchange.1 = (bf16[2048,128]{1,0:T(8,128)(2,1)S(1)}, bf16[2048,128]{1,0:T(8,128)(2,1)S(1)}, bf16[4,512,128]{2,1,0:T(8,128)(2,1)S(1)}, bf16[4,512,128]{2,1,0:T(8...) custom-call(bf16[2048,128]{1,0:T(8,128)(2,1)S(1)} %bitcast.12, bf16[2048,128]{1,0:T(8,128)(2,1)S(1)} %bitcast.13, ...), custom_call_target="tpu_custom_call" | custom-call | tf_op jit(solution)/shard_map/exchange/pallas_call | solution.py:298
  57.6 12.5 %compute.1 = (bf16[2048,256]{1,0:T(8,128)(2,1)}, bf16[2048,256]{1,0:T(8,128)(2,1)}) custom-call(bf16[2048,128]{1,0:T(8,128)(2,1)S(1)} %get-tuple-element.10.u, bf16[2048,128]{1,0:T(8,128)(2,1)S(1)} %get-tuple-element.11.v, bf16[2048,128]{1,0:T(8,128)(2,1)S(1)} %bitcast.14, bf16[2048,128]{1,0:T(8,128)(2,1)S(1)} %bitcast.15, ...), custom_call_target="tpu_custom_call" | custom-call | tf_op jit(solution)/shard_map/compute/pallas_call | solution.py:319
  (1 shorter events, 0.0 us)
Async XLA Ops:
  2.0 1.0 %copy-start = (bf16[1,1,2048,128]{3,2,1,0:T(8,128)(2,1)S(1)}, bf16[1,1,2048,128]{3,2,1,0:T(8,128)(2,1)}, u32[]{:S(2)}) copy-start(bf16[1,1,2048,128]{3,2,1,0:T(8,128)(2,1)} %param.6) | copy-start | bytes 1572868
  3.0 1.0 %copy-start.1 = (bf16[1,1,2048,128]{3,2,1,0:T(8,128)(2,1)S(1)}, bf16[1,1,2048,128]{3,2,1,0:T(8,128)(2,1)}, u32[]{:S(2)}) copy-start(bf16[1,1,2048,128]{3,2,1,0:T(8,128)(2,1)} %param.7) | copy-start | bytes 1572868
  4.1 0.9 %copy-start.2 = (bf16[2,1,512,128]{3,2,1,0:T(8,128)(2,1)S(1)}, bf16[2,1,512,128]{3,2,1,0:T(8,128)(2,1)}, u32[]{:S(2)}) copy-start(bf16[2,1,512,128]{3,2,1,0:T(8,128)(2,1)} %param.9) | copy-start | bytes 786436
  5.0 0.9 %copy-start.3 = (bf16[2,1,512,128]{3,2,1,0:T(8,128)(2,1)S(1)}, bf16[2,1,512,128]{3,2,1,0:T(8,128)(2,1)}, u32[]{:S(2)}) copy-start(bf16[2,1,512,128]{3,2,1,0:T(8,128)(2,1)} %param.10) | copy-start | bytes 786436

commit v2 on v1

--- a/solution.py
+++ b/solution.py
@@ -13,19 +13,32 @@
 F32 = jnp.float32
 
 
-def exchange(R, C, u, v, pleft, pright, meta, uo, vo, rowo, colo, coupo, metao,
-             ubuf, vbuf, rowbuf, colbuf, prbuf, psend, precv, mbuf,
-             s_swap, r_swap, s_row, r_row, s_col, r_col, s_st, s_pr, r_pr, s_part, r_part, s_meta, r_meta, s_loc):
+def exchange(R, C, u, v, pleft, pright, meta, stack, pair, uph, upm, inh, inm,
+             ubuf, vbuf, uown, vown, pr1, rowbuf, colbuf, prbuf, psend, precv, mbuf, work,
+             s_swap, r_swap, s_row, r_row, s_fwd, s_col, r_col, s_st, s_pr, r_pr, s_part, r_part, s_meta, r_meta,
+             s_loc):
     r, c = lax.axis_index("row"), lax.axis_index("col")
     half = C // 2
     mate = lax.rem(c + half, C)
     sib = r + 1 - 2 * lax.rem(r, 2)
     has_up, has_dn = r + 2 < R, r >= 2
+    nb, rk = u.shape
+    blk, rp = pleft.shape[1:]
+    n = rk + rp
 
     def rcopy(src, dst, ss, rs, to):
         return pltpu.make_async_remote_copy(
             src_ref=src, dst_ref=dst, send_sem=ss, recv_sem=rs, device_id=to, device_id_type=MESH
         )
+
+    load_u = pltpu.make_async_copy(u, uown, s_loc.at[3])
+    load_v = pltpu.make_async_copy(v, vown, s_loc.at[4])
+    load_r = pltpu.make_async_copy(pright.at[1], pr1, s_loc.at[5])
+    load_l = pltpu.make_async_copy(pleft.at[1], rowbuf.at[c], s_loc.at[6])
+    load_r.start()
+    load_l.start()
+    load_u.start()
+    load_v.start()
 
     barrier = pltpu.get_barrier_semaphore()
     for d in range(C):
@@ -89,12 +102,17 @@
             copy.start()
 
     for d in range(C):
-        send(c != d, rcopy(pleft.at[1], rowbuf.at[c], s_row.at[d], r_row.at[c], (r, d)))
-
+        same = (c // half) == d // half
+        send((c != d) & (same | (mate == d)),
+             rcopy(pleft.at[1], rowbuf.at[c], s_row.at[d], r_row.at[c], (r, d)))
     swap_u = rcopy(u, ubuf, s_swap.at[0], r_swap.at[0], (r, mate))
     swap_v = rcopy(v, vbuf, s_swap.at[1], r_swap.at[1], (r, mate))
     swap_u.start()
-    swap_v.start()
+
+    rcopy(pleft.at[1], rowbuf.at[mate], s_row.at[0], r_row.at[mate], (r, mate)).wait_recv()
+    for d in range(C):
+        same = (c // half) == d // half
+        send((c != d) & same, rcopy(rowbuf.at[mate], rowbuf.at[mate], s_fwd.at[d], r_row.at[mate], (r, d)))
 
     for s in range(C):
         slot, rs, ss = prbuf.at[s], r_pr.at[s], s_pr.at[s]
@@ -121,8 +139,9 @@
         def _():
             mbuf[d] = meta[...]
 
+    load_r.wait()
     part = [
-        lax.dot_general(pright[1], prbuf[s], (((0,), (0,)), ((), ())), preferred_element_type=F32)
+        lax.dot_general(pr1[...], prbuf[s], (((0,), (0,)), ((), ())), preferred_element_type=F32)
         for s in range(C)
     ]
     for d in range(C):
@@ -135,6 +154,8 @@
             precv[d] = value
     for d in range(C):
         send(c != d, rcopy(psend.at[d], precv.at[c], s_part.at[d], r_part.at[c], (r, d)))
+
+    swap_v.start()
 
     for b in range(C):
         for t in range(2):
@@ -153,24 +174,18 @@
 
     own_meta = meta[...]
     flagged = own_meta[0:1, :] > 0.5
-
-    for d in range(C):
-        @pl.when(c != d)
+    chosen_meta = jnp.where(flagged, mbuf[mate], own_meta)
+    lane = lax.broadcasted_iota(jnp.int32, (1, rk), 1).astype(F32)
+    live = lane < chosen_meta[1:2, :] * RBLK
+    zero = jnp.zeros((), BF16)
+
+    load_l.wait()
+    for d in range(C):
+        @pl.when((c != d) & (mate != d))
         def _():
             rcopy(pleft.at[1], rowbuf.at[d], s_row.at[d], r_row.at[d], (r, d)).wait_recv()
-            rowo[d] = rowbuf[d]
-
-        @pl.when(c == d)
-        def _():
-            rowo[d] = pleft[1]
-
-    for b in range(C):
-        colo[b] = jnp.where(flagged, colbuf[1, b], colbuf[0, b])
-
+    load_u.wait()
     swap_u.wait_recv()
-    uo[...] = jnp.where(flagged, ubuf[...], u[...])
-    swap_v.wait_recv()
-    vo[...] = jnp.where(flagged, vbuf[...], v[...])
     for d in range(C):
         @pl.when(c != d)
         def _():
@@ -178,8 +193,39 @@
     total = precv[0]
     for d in range(1, C):
         total = total + precv[d]
-    coupo[...] = total.astype(BF16)
-    metao[...] = jnp.where(flagged, mbuf[mate], own_meta)
+    coup = total.astype(BF16)
+
+    def fill(step, acc):
+        at = pl.ds(pl.multiple_of(step * blk, blk), blk)
+        lifted = -jnp.dot(rowbuf[step], coup, preferred_element_type=F32)
+        left = jnp.where(flagged, ubuf[at, :], uown[at, :])
+        piece = jnp.concatenate([jnp.where(live, left, zero), lifted.astype(BF16)], axis=1)
+        stack[at, :] = piece
+        return acc + lax.dot_general(piece, piece, (((0,), (0,)), ((), ())), preferred_element_type=F32)
+
+    gram = lax.fori_loop(0, C, fill, jnp.zeros((n, n), F32)) / nb
+    ri = lax.broadcasted_iota(jnp.int32, (n, n), 0)
+    ci = lax.broadcasted_iota(jnp.int32, (n, n), 1)
+    dead = jnp.concatenate([jnp.where(live, 0.0, 1.0).astype(F32), jnp.zeros((1, rp), F32)], axis=1)
+    work[:, :n] = gram + jnp.where(ri == ci, dead, 0.0)
+    work[:, n:] = jnp.where(ri == ci, 1.0, 0.0).astype(F32)
+    factor_rows(work, n, 32)
+    upper = jnp.where(ri <= ci, work[:, :n], 0.0)
+    inverse = work[:, n:]
+    uph[...], upm[...], _ = split3(upper)
+    inh[...], inm[...], _ = split3(inverse)
+
+    load_v.wait()
+    swap_v.wait_recv()
+
+    def fill_right(step, _):
+        at = pl.ds(pl.multiple_of(step * blk, blk), blk)
+        right = jnp.where(flagged, vbuf[at, :], vown[at, :])
+        own = jnp.where(flagged, colbuf[1, step], colbuf[0, step])
+        pair[at, :] = jnp.concatenate([jnp.where(live, right, zero), own], axis=1)
+        return 0
+
+    lax.fori_loop(0, C, fill_right, 0)
 
     swap_u.wait_send()
     swap_v.wait_send()
@@ -243,88 +289,57 @@
             work[r1:n, a0 : a0 + width] = work[r1:n, a0 : a0 + width] - update[r1 - b0 :, :]
 
 
-def compute(chunk, u, v, row, col, coup, meta, lo, ro, stack, work):
-    nb, rk = u.shape
-    rp = coup.shape[1]
-    n = rk + rp
-    lane = lax.broadcasted_iota(jnp.int32, (1, rk), 1).astype(F32)
-    live = lane < meta[1:2, :] * RBLK
-
-    def fill(step, acc):
-        at = pl.ds(pl.multiple_of(step * chunk, chunk), chunk)
-        lifted = -jnp.dot(row[at, :], coup[...], preferred_element_type=F32)
-        piece = jnp.concatenate(
-            [jnp.where(live, u[at, :], jnp.zeros((), BF16)), lifted.astype(BF16)], axis=1
-        )
-        stack[at, :] = piece
-        return acc + lax.dot_general(piece, piece, (((0,), (0,)), ((), ())), preferred_element_type=F32)
-
-    gram = lax.fori_loop(0, nb // chunk, fill, jnp.zeros((n, n), F32)) / nb
-    ri = lax.broadcasted_iota(jnp.int32, (n, n), 0)
-    ci = lax.broadcasted_iota(jnp.int32, (n, n), 1)
-    dead = jnp.concatenate([jnp.where(live, 0.0, 1.0).astype(F32), jnp.zeros((1, rp), F32)], axis=1)
-    work[:, :n] = gram + jnp.where(ri == ci, dead, 0.0)
-    work[:, n:] = jnp.where(ri == ci, 1.0, 0.0).astype(F32)
-    factor_rows(work, n, 32)
-    upper = jnp.where(ri <= ci, work[:, :n], 0.0)
-    inverse = work[:, n:]
-    uh, um, _ = split3(upper)
-    ih, im, _ = split3(inverse)
+def products(x, y, uph, upm, inh, inm, lo, ro):
     nt = (((1,), (1,)), ((), ()))
-
-    def emit(step, _):
-        at = pl.ds(pl.multiple_of(step * chunk, chunk), chunk)
-        x = stack[at, :]
-        left = lax.dot_general(x, ih, nt, preferred_element_type=F32)
-        left = left + lax.dot_general(x, im, nt, preferred_element_type=F32)
-        lo[at, :] = left.astype(BF16)
-        y = jnp.concatenate([jnp.where(live, v[at, :], jnp.zeros((), BF16)), col[at, :]], axis=1)
-        right = lax.dot_general(y, uh, nt, preferred_element_type=F32)
-        right = right + lax.dot_general(y, um, nt, preferred_element_type=F32)
-        ro[at, :] = right.astype(BF16)
-        return 0
-
-    lax.fori_loop(0, nb // chunk, emit, 0)
+    chunk = lo.shape[0]
+    at = pl.ds(pl.multiple_of(pl.program_id(0) * chunk, chunk), chunk)
+
+    def product(value, high, low):
+        out = lax.dot_general(value, high[...], nt, preferred_element_type=F32)
+        return (out + lax.dot_general(value, low[...], nt, preferred_element_type=F32)).astype(BF16)
+
+    lo[...] = product(x[at, :], inh, inm)
+    ro[...] = product(y[at, :], uph, upm)
 
 
 def per_device(R, C, tile_left, tile_right, tile_blocks, panel_left, panel_right, swap_flag):
     nb, rk = tile_left.shape[2:]
     blk, rp = panel_left.shape[2:]
+    n = rk + rp
     top = lax.broadcasted_iota(jnp.int32, (8, 128), 0) == 0
     meta = jnp.where(top, swap_flag[0, 0], tile_blocks[0, 0]).astype(F32)
     vm = pl.BlockSpec(memory_space=pltpu.VMEM)
+    hbm = pl.BlockSpec(memory_space=pltpu.HBM)
     dma = pltpu.SemaphoreType.DMA
     S = jax.ShapeDtypeStruct
-    uo, vo, rowo, colo, coup, metao = pl.pallas_call(
+    V = pltpu.VMEM
+    parts = pl.pallas_call(
         functools.partial(exchange, R, C),
-        out_shape=(
-            S((nb, rk), BF16), S((nb, rk), BF16), S((C, blk, rp), BF16), S((C, blk, rp), BF16),
-            S((rp, rp), BF16), S((8, 128), F32),
-        ),
-        in_specs=[vm] * 5,
+        out_shape=(S((nb, n), BF16),) * 2 + (S((n, n), BF16),) * 4,
+        in_specs=[hbm] * 4 + [vm],
         out_specs=[vm] * 6,
         scratch_shapes=[
-            pltpu.VMEM((nb, rk), BF16), pltpu.VMEM((nb, rk), BF16),
-            pltpu.VMEM((C, blk, rp), BF16), pltpu.VMEM((2, C, blk, rp), BF16), pltpu.VMEM((C, blk, rp), BF16),
-            pltpu.VMEM((C, rp, rp), F32), pltpu.VMEM((C, rp, rp), F32), pltpu.VMEM((C, 8, 128), F32),
-            dma((2,)), dma((2,)), dma((C,)), dma((C,)), dma((2, C, 3)), dma((2, C)), dma((2,)),
-            dma((C, 3)), dma((C,)), dma((C,)), dma((C,)), dma((C,)), dma((C,)), dma((3,)),
+            V((nb, rk), BF16), V((nb, rk), BF16), V((nb, rk), BF16), V((nb, rk), BF16), V((blk, rp), BF16),
+            V((C, blk, rp), BF16), V((2, C, blk, rp), BF16), V((C, blk, rp), BF16),
+            V((C, rp, rp), F32), V((C, rp, rp), F32), V((C, 8, 128), F32), V((n, 2 * n), F32),
+            dma((2,)), dma((2,)), dma((C,)), dma((C,)), dma((C,)), dma((2, C, 3)), dma((2, C)), dma((2,)),
+            dma((C, 3)), dma((C,)), dma((C,)), dma((C,)), dma((C,)), dma((C,)), dma((7,)),
         ],
         compiler_params=pltpu.CompilerParams(
-            collective_id=0, has_side_effects=True, vmem_limit_bytes=40 * 1024 * 1024
+            collective_id=0, has_side_effects=True, vmem_limit_bytes=24 * 1024 * 1024
         ),
         name="exchange",
     )(tile_left[0, 0], tile_right[0, 0], panel_left[:, 0], panel_right[:, 0], meta)
-    n = rk + rp
+    piece = pl.BlockSpec((min(512, nb), n), lambda i: (i, 0))
     lo, ro = pl.pallas_call(
-        functools.partial(compute, min(512, nb)),
-        out_shape=(S((nb, n), BF16), S((nb, n), BF16)),
+        products,
+        grid=(nb // min(512, nb),),
+        out_shape=(S((nb, n), BF16),) * 2,
         in_specs=[vm] * 6,
-        out_specs=[vm] * 2,
-        scratch_shapes=[pltpu.VMEM((nb, n), BF16), pltpu.VMEM((n, 2 * n), F32)],
-        compiler_params=pltpu.CompilerParams(vmem_limit_bytes=40 * 1024 * 1024),
-        name="compute",
-    )(uo, vo, rowo.reshape(nb, rp), colo.reshape(nb, rp), coup, metao)
+        out_specs=[piece] * 2,
+        compiler_params=pltpu.CompilerParams(vmem_limit_bytes=24 * 1024 * 1024),
+        name="products",
+    )(*parts)
     return lo[None, None], ro[None, None]
 
 

time: 70.4 us -> 74.5 us (1.058)
  Pallas kernels: 64.1 us -> 68.2 us
    pallas_call x2, Pallas kernels: 64.1 us -> 68.2 us  [the longest x1 65.2 us: per_device(): pl.pallas_call(functools.partial(exchange, R, C), out_shape=(S((nb, n), B...]
where the time goes in v2:
time: 74.5 us; the launch traced here: 74.2 us
  Pallas kernels  68.2 us (92%)
  local copies, waits for them, and re-layouts  4.05 us (5%)
  between operations  1.94 us (3%)
    pallas_call x1, Pallas kernels, per_device(): pl.pallas_call(functools.partial(exchange, R, C), out_shape=(S((nb, n), B...  65.2 us
    unnamed x8, local copies, waits for them, and re-layouts  3.98 us
    pallas_call x1, Pallas kernels, per_device(): pl.pallas_call(products, grid=(nb // min(512, nb),), out_shape=(S((nb, n)...  3.03 us

profile of v2, /device:TPU:29, one launch (start us, length us, event | category | flops | bytes accessed | tf_op | source)
XLA Modules:
  0.0 74.2 jit_solution(2121544751832950849)
XLA Ops:
  1.9 0.1 iota.7.meta
  2.0 0.0 copy-start
  2.0 1.0 %copy-done = bf16[1,1,2048,128]{3,2,1,0:T(8,128)(2,1)S(1)} copy-done((bf16[1,1,2048,128]{3,2,1,0:T(8,128)(2,1)S(1)}, bf16[1,1,2048,128]{3,2,1,0:T(8,128)(2,1)}, u32[]{:S(2)}) %copy-start) | copy-done | bytes 524312
  3.0 0.0 copy-start.1
  3.0 1.0 %copy-done.1 = bf16[1,1,2048,128]{3,2,1,0:T(8,128)(2,1)S(1)} copy-done((bf16[1,1,2048,128]{3,2,1,0:T(8,128)(2,1)S(1)}, bf16[1,1,2048,128]{3,2,1,0:T(8,128)(2,1)}, u32[]{:S(2)}) %copy-start.1) | copy-done | bytes 524312
  4.1 0.0 copy-start.2
  4.1 0.9 %copy-done.2 = bf16[2,1,512,128]{3,2,1,0:T(8,128)(2,1)S(1)} copy-done((bf16[2,1,512,128]{3,2,1,0:T(8,128)(2,1)S(1)}, bf16[2,1,512,128]{3,2,1,0:T(8,128)(2,1)}, u32[]{:S(2)}) %copy-start.2) | copy-done | bytes 262168
  5.0 0.0 copy-start.3
  5.0 0.9 %copy-done.3 = bf16[2,1,512,128]{3,2,1,0:T(8,128)(2,1)S(1)} copy-done((bf16[2,1,512,128]{3,2,1,0:T(8,128)(2,1)S(1)}, bf16[2,1,512,128]{3,2,1,0:T(8,128)(2,1)}, u32[]{:S(2)}) %copy-start.3) | copy-done | bytes 262168
  6.0 65.2 %exchange.1 = (bf16[2048,256]{1,0:T(8,128)(2,1)S(1)}, bf16[2048,256]{1,0:T(8,128)(2,1)S(1)}, bf16[256,256]{1,0:T(8,128)(2,1)S(1)}, bf16[256,256]{1,0:T(8,128)(2,...) custom-call(bf16[2048,128]{1,0:T(8,128)(2,1)S(1)} %bitcast.10, bf16[2048,128]{1,0:T(8,128)(2,1)S(1)} %bitcast.11, ...), custom_call_target="tpu_custom_call" | custom-call | tf_op jit(solution)/shard_map/exchange/pallas_call | solution.py:316
  71.2 3.0 %products.1 = (bf16[2048,256]{1,0:T(8,128)(2,1)}, bf16[2048,256]{1,0:T(8,128)(2,1)}) custom-call(bf16[2048,256]{1,0:T(8,128)(2,1)S(1)} %get-tuple-element.10.x, bf16[2048,256]{1,0:T(8,128)(2,1)S(1)} %get-tuple-element.11.y, bf16[256,256]{1,0:T(8,128)(2,1)S(1)} %get-tuple-element.12.uph, bf16[256,256]{1,0:T(8,128)(2,1)S(1)} %get-tuple-element.13.upm, ...), custom_call_target="tpu_custom_call" | custom-call | tf_op jit(solution)/shard_map/products/pallas_call | solution.py:334
  (1 shorter events, 0.0 us)
Async XLA Ops:
  2.0 1.0 %copy-start = (bf16[1,1,2048,128]{3,2,1,0:T(8,128)(2,1)S(1)}, bf16[1,1,2048,128]{3,2,1,0:T(8,128)(2,1)}, u32[]{:S(2)}) copy-start(bf16[1,1,2048,128]{3,2,1,0:T(8,128)(2,1)} %param.6) | copy-start | bytes 1572868
  3.0 1.0 %copy-start.1 = (bf16[1,1,2048,128]{3,2,1,0:T(8,128)(2,1)S(1)}, bf16[1,1,2048,128]{3,2,1,0:T(8,128)(2,1)}, u32[]{:S(2)}) copy-start(bf16[1,1,2048,128]{3,2,1,0:T(8,128)(2,1)} %param.7) | copy-start | bytes 1572868
  4.1 0.9 %copy-start.2 = (bf16[2,1,512,128]{3,2,1,0:T(8,128)(2,1)S(1)}, bf16[2,1,512,128]{3,2,1,0:T(8,128)(2,1)}, u32[]{:S(2)}) copy-start(bf16[2,1,512,128]{3,2,1,0:T(8,128)(2,1)} %param.9) | copy-start | bytes 786436
  5.0 0.9 %copy-start.3 = (bf16[2,1,512,128]{3,2,1,0:T(8,128)(2,1)S(1)}, bf16[2,1,512,128]{3,2,1,0:T(8,128)(2,1)}, u32[]{:S(2)}) copy-start(bf16[2,1,512,128]{3,2,1,0:T(8,128)(2,1)} %param.10) | copy-start | bytes 786436

commit v3 on v2

--- a/solution.py
+++ b/solution.py
@@ -107,12 +107,6 @@
              rcopy(pleft.at[1], rowbuf.at[c], s_row.at[d], r_row.at[c], (r, d)))
     swap_u = rcopy(u, ubuf, s_swap.at[0], r_swap.at[0], (r, mate))
     swap_v = rcopy(v, vbuf, s_swap.at[1], r_swap.at[1], (r, mate))
-    swap_u.start()
-
-    rcopy(pleft.at[1], rowbuf.at[mate], s_row.at[0], r_row.at[mate], (r, mate)).wait_recv()
-    for d in range(C):
-        same = (c // half) == d // half
-        send((c != d) & same, rcopy(rowbuf.at[mate], rowbuf.at[mate], s_fwd.at[d], r_row.at[mate], (r, d)))
 
     for s in range(C):
         slot, rs, ss = prbuf.at[s], r_pr.at[s], s_pr.at[s]
@@ -125,6 +119,13 @@
         send(par & (r > s) & has_up, rcopy(slot, slot, ss.at[0], rs, (r + 2, c)))
         send(par & (r < s) & has_dn, rcopy(slot, slot, ss.at[1], rs, (r - 2, c)))
         send(par & (r != s), rcopy(slot, slot, ss.at[2], rs, (sib, c)))
+
+    rcopy(pleft.at[1], rowbuf.at[mate], s_row.at[0], r_row.at[mate], (r, mate)).wait_recv()
+    for d in range(C):
+        same = (c // half) == d // half
+        send((c != d) & same, rcopy(rowbuf.at[mate], rowbuf.at[mate], s_fwd.at[d], r_row.at[mate], (r, d)))
+
+    swap_u.start()
 
     @pl.when(is_src_pr)
     def _():
@@ -291,15 +292,13 @@
 
 def products(x, y, uph, upm, inh, inm, lo, ro):
     nt = (((1,), (1,)), ((), ()))
-    chunk = lo.shape[0]
-    at = pl.ds(pl.multiple_of(pl.program_id(0) * chunk, chunk), chunk)
 
     def product(value, high, low):
         out = lax.dot_general(value, high[...], nt, preferred_element_type=F32)
         return (out + lax.dot_general(value, low[...], nt, preferred_element_type=F32)).astype(BF16)
 
-    lo[...] = product(x[at, :], inh, inm)
-    ro[...] = product(y[at, :], uph, upm)
+    lo[...] = product(x[...], inh, inm)
+    ro[...] = product(y[...], uph, upm)
 
 
 def per_device(R, C, tile_left, tile_right, tile_blocks, panel_left, panel_right, swap_flag):
@@ -326,7 +325,7 @@
             dma((C, 3)), dma((C,)), dma((C,)), dma((C,)), dma((C,)), dma((C,)), dma((7,)),
         ],
         compiler_params=pltpu.CompilerParams(
-            collective_id=0, has_side_effects=True, vmem_limit_bytes=24 * 1024 * 1024
+            collective_id=0, has_side_effects=True, vmem_limit_bytes=58 * 1024 * 1024
         ),
         name="exchange",
     )(tile_left[0, 0], tile_right[0, 0], panel_left[:, 0], panel_right[:, 0], meta)
@@ -335,9 +334,8 @@
         products,
         grid=(nb // min(512, nb),),
         out_shape=(S((nb, n), BF16),) * 2,
-        in_specs=[vm] * 6,
+        in_specs=[piece] * 2 + [pl.BlockSpec((n, n), lambda i: (0, 0))] * 4,
         out_specs=[piece] * 2,
-        compiler_params=pltpu.CompilerParams(vmem_limit_bytes=24 * 1024 * 1024),
         name="products",
     )(*parts)
     return lo[None, None], ro[None, None]

time: 74.5 us -> 70.1 us (0.941)
  local copies, waits for them, and re-layouts: 4.05 us -> 0.66 us
  Pallas kernels: 68.2 us -> 67.3 us
    unnamed x8 -> x0, local copies, waits for them, and re-layouts: 3.98 us -> none
    pallas_call x1, Pallas kernels: 65.2 us -> 62.5 us  [per_device(): pl.pallas_call(functools.partial(exchange, R, C), out_shape=(S((nb, n), B...]
    pallas_call x1, Pallas kernels: 3.03 us -> 4.8 us  [per_device(): pl.pallas_call(products, grid=(nb // min(512, nb),), out_shape=(S((nb, n)...]
where the time goes in v3:
time: 70.1 us; the launch traced here: 69.9 us
  Pallas kernels  67.3 us (96%)
  between operations  1.94 us (3%)
    pallas_call x1, Pallas kernels, per_device(): pl.pallas_call(functools.partial(exchange, R, C), out_shape=(S((nb, n), B...  62.5 us
    pallas_call x1, Pallas kernels, per_device(): pl.pallas_call(products, grid=(nb // min(512, nb),), out_shape=(S((nb, n)...  4.8 us

profile of v3, /device:TPU:29, one launch (start us, length us, event | category | flops | bytes accessed | tf_op | source)
XLA Modules:
  0.0 69.9 jit_solution(17768471777900776890)
XLA Ops:
  1.9 0.7 iota.7.meta
  2.6 62.5 %exchange.1 = (bf16[2048,256]{1,0:T(8,128)(2,1)}, bf16[2048,256]{1,0:T(8,128)(2,1)}, bf16[256,256]{1,0:T(8,128)(2,1)}, bf16[256,256]{1,0:T(8,128)(2,1)}, bf16[25...) custom-call(bf16[2048,128]{1,0:T(8,128)(2,1)} %bitcast.10, bf16[2048,128]{1,0:T(8,128)(2,1)} %bitcast.11, ...), custom_call_target="tpu_custom_call" | custom-call | tf_op jit(solution)/shard_map/exchange/pallas_call | solution.py:315
  65.1 4.8 %products.1 = (bf16[2048,256]{1,0:T(8,128)(2,1)}, bf16[2048,256]{1,0:T(8,128)(2,1)}) custom-call(bf16[2048,256]{1,0:T(8,128)(2,1)} %get-tuple-element.10.x, bf16[2048,256]{1,0:T(8,128)(2,1)} %get-tuple-element.11.y, bf16[256,256]{1,0:T(8,128)(2,1)} %get-tuple-element.12.uph, bf16[256,256]{1,0:T(8,128)(2,1)} %get-tuple-element.13.upm, ...), custom_call_target="tpu_custom_call" | custom-call | tf_op jit(solution)/shard_map/products/pallas_call | solution.py:333
  (1 shorter events, 0.0 us)
